TPU v7x, 32 devices: a whole 2x2x4 slice. The times are simulated.
32 devices in a mesh: tm: 4 (over y, x), paths: 8 (over z, core).
Axes of the slice: x: 2, y: 2, z: 4, core: 2. Of those that a mesh axis runs over, the one named last changes fastest.
Arguments:
- returns: bfloat16 [128, 4096, 256], P('tm', 'paths'), may hold values from -0.15917969 to 0.15917969
- weights: bfloat16 [256, 64], P('paths'), may hold values from -0.375 to 0.375
Outputs:
- drawdown: float32 [64, 4096], P('tm', 'paths')
All inputs are finite; a program needn't handle non-finite values.
Results may differ from a plain program's by a relative error of at most 0.0003.
Values may be sent and summed in bfloat16 or wider, within the bound.
A program may use at most 64 MiB of HBM per device.

v0:
```python
import jax
import jax.numpy as jnp
from jax import lax
from jax.sharding import PartitionSpec as P

very_large = 1e30


def prefix(part, axis, combine, identity):
    place = lax.axis_index(axis)
    gathered = jax.tree.map(lambda a: lax.all_gather(a, axis), part)
    state = jax.tree.map(lambda a, e: jnp.zeros_like(a) + jnp.asarray(e, a.dtype), part, identity)

    def one(lap, state):
        return combine(
            state, jax.tree.map(lambda a: lax.dynamic_index_in_dim(a, lap, 0, False), gathered)
        )

    return lax.fori_loop(0, place, one, state)


def join_two(earlier, later):
    return (earlier[0] + later[0], jnp.maximum(earlier[1], earlier[0] + later[1]))


def shards(returns, weights):
    all_weights = lax.all_gather(weights, "paths", axis=0, tiled=True)
    profit = jnp.einsum("tpa,aq->tqp", returns, all_weights, preferred_element_type=jnp.float32)
    steps_here = profit.shape[0]
    row_ids = lax.broadcasted_iota(jnp.int32, (steps_here, steps_here), 0)
    col_ids = lax.broadcasted_iota(jnp.int32, (steps_here, steps_here), 1)
    lower = (row_ids >= col_ids).astype(jnp.float32)
    flat = profit.reshape(steps_here, -1)
    values = jnp.dot(
        lower, flat, precision=lax.Precision.HIGHEST, preferred_element_type=jnp.float32
    ).reshape(profit.shape)
    peaks = jnp.maximum(lax.cummax(values, axis=0), 0.0)
    offset = values[-1]
    highest = peaks[-1]
    segments = lax.axis_size("tm")
    block_width = offset.shape[0] // segments
    zeros = jnp.zeros_like(offset)
    prior_offset, prior_peak = prefix(
        (offset, highest), "tm", join_two, (zeros, zeros - very_large)
    )
    running = jnp.maximum(prior_peak[None], prior_offset[None] + peaks)
    falls = jnp.max(running - (prior_offset[None] + values), axis=0)
    blocks = falls.reshape(segments, block_width, falls.shape[1])
    received = lax.all_to_all(blocks, "tm", split_axis=0, concat_axis=0, tiled=True)
    return jnp.max(received, axis=0)


def solution(mesh):
    in_specs = (P("tm", "paths", None), P("paths", None))
    out_specs = P("tm", "paths")
    return jax.shard_map(shards, mesh=mesh, in_specs=in_specs, out_specs=out_specs, check_vma=False)
```

profile of v0, /device:TPU:0, one launch (start us, length us, event | category | flops | bytes accessed | tf_op | source)
XLA Modules:
  0.0 87.8 jit_solution(8947005105098982368)
XLA Ops:
  0.0 15.9 %all_gather.9 = bf16[256,64]{1,0:T(8,128)(2,1)S(1)} all-gather(bf16[32,64]{1,0:T(8,128)(2,1)} %param.5), channel_id=1, replica_groups=mesh['tm'=4,'paths'=8] {'paths'}, dimensions={0}, use_global_device_ids=true | all-gather | bytes 36864 | tf_op jit(solution)/shard_map/all_gather | solution.py:27
  15.9 6.0 %fusion.1 = f32[64,32,512]{2,0,1:T(8,128)S(1)} fusion(bf16[32,512,256]{2,1,0:T(8,128)(2,1)} %param.4, bf16[256,64]{1,0:T(8,128)(2,1)S(1)} %all_gather.9), kind=kOutput, calls=%fused_computation.6 | convolution fusion | flops 536870912 | bytes 12615680 | tf_op jit(solution)/shard_map/tpa,aq->tqp/dot_general | solution.py:28
  21.9 2.4 %copy.3 = f32[4,8,64,512]{3,1,2,0:T(8,128)S(1)} copy(f32[4,8,64,512]{3,2,1,0:T(8,128)S(1)} %bitcast.27) | data formatting | bytes 8388608
  24.4 2.1 %fusion.3 = f32[32,32768]{1,0:T(8,128)S(1)} fusion(f32[32,32768]{1,0:T(8,128)S(1)} %bitcast.29), kind=kOutput, calls=%fused_computation.9 | convolution fusion | flops 402654208 | bytes 8388608 | tf_op jit(solution)/shard_map/dot_general | solution.py:34
  26.5 0.0 copy-start
  26.5 0.4 slice_reduce_fusion
  26.9 2.4 %copy.4 = f32[4,8,64,512]{3,2,1,0:T(8,128)S(1)} copy(f32[4,8,64,512]{3,1,2,0:T(8,128)S(1)} %bitcast.25) | data formatting | bytes 8388608
  29.3 0.0 copy-done
  29.3 20.9 %broadcast_maximum_fusion = f32[32,64,512]{2,1,0:T(8,128)S(1)} fusion(f32[32,64,512]{2,1,0:T(8,128)S(1)} %bitcast.30), kind=kOutput, calls=%fused_computation.4 | output fusion | flops 33554432 | bytes 8388608 | tf_op jit(solution)/shard_map/shards/reduce_window_max | solution.py:37
  50.2 0.0 copy-start.2
  50.2 2.0 %copy-done.2 = f32[32,64,512]{2,1,0:T(8,128)} copy-done((f32[32,64,512]{2,1,0:T(8,128)}, f32[32,64,512]{2,1,0:T(8,128)S(1)}, u32[]{:S(2)}) %copy-start.2) | copy-done | bytes 4194328
  52.2 10.3 %all_gather.11 = f32[4,64,512]{2,1,0:T(8,128)S(1)} all-gather(f32[1,64,512]{2,1,0:T(8,128)S(1)} %slice.13), channel_id=1, replica_groups=mesh['tm'=4,'paths'=8] {'tm'}, dimensions={0}, use_global_device_ids=true | all-gather | bytes 655360 | tf_op jit(solution)/shard_map/all_gather | solution.py:11
  62.6 10.7 %all_gather.10 = f32[4,64,512]{2,1,0:T(8,128)S(1)} all-gather(f32[1,64,512]{2,1,0:T(8,128)S(1)} %slice.10), channel_id=1, replica_groups=mesh['tm'=4,'paths'=8] {'tm'}, dimensions={0}, use_global_device_ids=true | all-gather | bytes 655360 | tf_op jit(solution)/shard_map/all_gather | solution.py:11
  73.3 0.2 while.12
  73.6 0.0 copy-start.1
  73.6 4.8 %copy.7 = f32[4,8,64,512]{3,1,2,0:T(8,128)S(1)} copy(f32[4,8,64,512]{3,2,1,0:T(8,128)} %bitcast.26) | data formatting | bytes 8388608
  78.4 0.0 copy-done.1
  78.4 0.9 %subtract_reduce_fusion = f32[32768]{0:T(1024)S(1)} fusion(f32[32,32768]{1,0:T(8,128)S(1)} %copy-done.1, f32[32,32768]{1,0:T(8,128)S(1)} %bitcast.28, f32[32768]{0:T(1024)S(1)} %bitcast.33, f32[32768]{0:T(1024)S(1)} %bitcast.34), kind=kLoop, calls=%fused_computation.3 | loop fusion | flops 5210112 | bytes 8781824 | tf_op jit(solution)/shard_map/reduce_max | solution.py:47
  79.4 7.8 %all_to_all.5 = f32[4,16,512]{2,1,0:T(8,128)S(1)} all-to-all(f32[4,16,512]{2,1,0:T(8,128)S(1)} %reshape.24), channel_id=1, replica_groups=mesh['tm'=4,'paths'=8] {'tm'}, dimensions={0} | all-to-all | bytes 262144 | tf_op jit(solution)/shard_map/all_to_all | solution.py:49
  87.2 0.6 reduce_max.19
  (7 shorter events, 0.1 us)
Async XLA Ops:
  26.5 2.8 %copy-start = (f32[32,32768]{1,0:T(8,128)}, f32[32,32768]{1,0:T(8,128)S(1)}, u32[]{:S(2)}) copy-start(f32[32,32768]{1,0:T(8,128)S(1)} %fusion.3) | copy-start | bytes 12582916
  50.2 2.0 %copy-start.2 = (f32[32,64,512]{2,1,0:T(8,128)}, f32[32,64,512]{2,1,0:T(8,128)S(1)}, u32[]{:S(2)}) copy-start(f32[32,64,512]{2,1,0:T(8,128)S(1)} %broadcast_maximum_fusion) | copy-start | bytes 12582916
  73.6 4.8 %copy-start.1 = (f32[32,32768]{1,0:T(8,128)S(1)}, f32[32,32768]{1,0:T(8,128)}, u32[]{:S(2)}) copy-start(f32[32,32768]{1,0:T(8,128)} %copy-done) | copy-start | bytes 12582916
where the time goes:
time: 88.1 us; the launch traced here: 87.8 us
  blocking collectives  44.8 us (51%)
  other arithmetic  22.5 us (26%)
  local copies, waits for them, and re-layouts  12.1 us (14%)
  matrix products  8.14 us (9%)
    all_gather x2, blocking collectives, prefix(): gathered = jax.tree.map(lambda a: lax.all_gather(a, axis), part)  21 us
    another operation x1, other arithmetic, shards(): peaks = jnp.maximum(lax.cummax(values, axis=0), 0.0)  20.9 us
    all_gather x1, blocking collectives, shards(): all_weights = lax.all_gather(weights, 'paths', axis=0, tiled=True)  15.9 us
    unnamed x11, local copies, waits for them, and re-layouts  11.7 us
    all_to_all x1, blocking collectives, shards(): lax.all_to_all(blocks, 'tm', split_axis=0, concat_axis=0, tiled=True)  7.85 us
    dot_general x1, matrix products, shards(): jnp.einsum('tpa,aq->tqp', returns, all_weights, preferred_element_type=jn...  6.03 us
    dot_general x1, matrix products, shards(): jnp.dot(lower, flat, precision=lax.Precision.HIGHEST, preferred_element_t...  2.11 us

commit v1 on v0

v1 whole, which is shorter than its diff:
```python
import functools

import jax
import jax.numpy as jnp
from jax import lax
from jax.experimental import pallas as pl
from jax.experimental.pallas import tpu as pltpu
from jax.sharding import PartitionSpec as P

MESH = pl.DeviceIdType.MESH
CHUNKS = 2
GROUP = 8
ROWS = 32


def kernel(
    n_tm, n_paths, ret_hbm, w_ref, out_ref,
    ret, wbuf, prof, send, recv, load_sem, wsend_sem, wrecv_sem, send_sem, recv_sem,
):
    steps, paths, assets = ret.shape
    ports = w_ref.shape[1]
    block = ports // n_tm
    width = paths // CHUNKS
    half = width // 2
    groups = steps // GROUP
    tm = lax.axis_index("tm")
    me = lax.axis_index("paths")

    def load(c, g):
        part = (pl.ds(g * GROUP, GROUP), pl.ds(c * width, width))
        return pltpu.make_async_copy(ret_hbm.at[part], ret.at[part], load_sem.at[c, g])

    for c in range(CHUNKS):
        for g in range(groups):
            load(c, g).start()

    barrier = pltpu.get_barrier_semaphore()
    for d in range(1, n_paths):
        pl.semaphore_signal(
            barrier, inc=1, device_id=(tm, lax.rem(me + d, n_paths)), device_id_type=MESH
        )
    for d in range(1, n_tm):
        pl.semaphore_signal(
            barrier, inc=1, device_id=(lax.rem(tm + d, n_tm), me), device_id_type=MESH
        )
    pl.semaphore_wait(barrier, n_paths - 1 + n_tm - 1)

    def weight_copy(d):
        return pltpu.make_async_remote_copy(
            src_ref=w_ref,
            dst_ref=wbuf.at[me],
            send_sem=wsend_sem.at[d - 1],
            recv_sem=wrecv_sem.at[d - 1],
            device_id=(tm, lax.rem(me + d, n_paths)),
            device_id_type=MESH,
        )

    def weight_arrival(d):
        return pltpu.make_async_remote_copy(
            src_ref=w_ref,
            dst_ref=wbuf.at[lax.rem(me + n_paths - d, n_paths)],
            send_sem=wsend_sem.at[d - 1],
            recv_sem=wrecv_sem.at[d - 1],
            device_id=(tm, lax.rem(me + d, n_paths)),
            device_id_type=MESH,
        )

    for d in range(1, n_paths):
        weight_copy(d).start()
    wbuf[me] = w_ref[...]
    for d in range(1, n_paths):
        weight_arrival(d).wait_recv()

    held = wbuf[...].reshape(assets, ports)
    blank = jnp.zeros_like(held)
    both = jnp.concatenate(
        [jnp.concatenate([held, blank], axis=1), jnp.concatenate([blank, held], axis=1)], axis=0
    )

    def block_copy(c, d, slot):
        return pltpu.make_async_remote_copy(
            src_ref=send.at[c, lax.rem(tm + d, n_tm)],
            dst_ref=recv.at[c, slot],
            send_sem=send_sem.at[c, d - 1],
            recv_sem=recv_sem.at[c, d - 1],
            device_id=(lax.rem(tm + d, n_tm), me),
            device_id_type=MESH,
        )

    for c in range(CHUNKS):
        first = pl.ds(c * width, half)
        second = pl.ds(c * width + half, half)
        for g in range(groups):
            load(c, g).wait()
            when = pl.ds(g * GROUP, GROUP)
            left = ret[when, first, :].reshape(GROUP * half, assets)
            right = ret[when, second, :].reshape(GROUP * half, assets)
            prof[c, when] = jnp.dot(
                jnp.concatenate([left, right], axis=1), both, preferred_element_type=jnp.float32
            ).reshape(GROUP, half, 2 * ports)
        pieces = []
        for r in range(0, half, ROWS):
            value = prof[c, 0, pl.ds(r, ROWS)]
            high, low, fall = value, value, jnp.zeros_like(value)
            for t in range(1, steps):
                value = value + prof[c, t, pl.ds(r, ROWS)]
                high = jnp.maximum(high, value)
                low = jnp.minimum(low, value)
                fall = jnp.maximum(fall, high - value)
            pieces.append((value, high, fall, low))
        for k in range(4):
            whole = jnp.concatenate([piece[k] for piece in pieces], axis=0).T
            for b in range(n_tm):
                rows = b * block
                send[c, b, k, :, 0:half] = whole[rows : rows + block]
                send[c, b, k, :, half:width] = whole[ports + rows : ports + rows + block]
        for d in range(1, n_tm):
            block_copy(c, d, tm).start()
        recv[c, tm] = send[c, tm]

    for c in range(CHUNKS):
        for d in range(1, n_tm):
            block_copy(c, d, lax.rem(tm + n_tm - d, n_tm)).wait_recv()
        level = jnp.zeros((block, width), jnp.float32)
        peak, deepest = level, level
        for s in range(n_tm):
            deepest = jnp.maximum(deepest, recv[c, s, 2])
            deepest = jnp.maximum(deepest, peak - (level + recv[c, s, 3]))
            peak = jnp.maximum(peak, level + recv[c, s, 1])
            level = level + recv[c, s, 0]
        out_ref[:, pl.ds(c * width, width)] = deepest

    for d in range(1, n_paths):
        weight_copy(d).wait_send()
    for c in range(CHUNKS):
        for d in range(1, n_tm):
            block_copy(c, d, tm).wait_send()


def solution(mesh):
    n_tm, n_paths = mesh.shape["tm"], mesh.shape["paths"]

    def shards(returns, weights):
        steps, paths, assets = returns.shape
        share, ports = weights.shape
        block, width = ports // n_tm, paths // CHUNKS
        dma = pltpu.SemaphoreType.DMA
        return pl.pallas_call(
            functools.partial(kernel, n_tm, n_paths),
            out_shape=jax.ShapeDtypeStruct((block, paths), jnp.float32),
            in_specs=[
                pl.BlockSpec(memory_space=pl.ANY),
                pl.BlockSpec(memory_space=pltpu.VMEM),
            ],
            out_specs=pl.BlockSpec(memory_space=pltpu.VMEM),
            scratch_shapes=[
                pltpu.VMEM((steps, paths, assets), returns.dtype),
                pltpu.VMEM((n_paths, share, ports), weights.dtype),
                pltpu.VMEM((CHUNKS, steps, width // 2, 2 * ports), jnp.float32),
                pltpu.VMEM((CHUNKS, n_tm, 4, block, width), jnp.float32),
                pltpu.VMEM((CHUNKS, n_tm, 4, block, width), jnp.float32),
                dma((CHUNKS, steps // GROUP)),
                dma((n_paths - 1,)),
                dma((n_paths - 1,)),
                dma((CHUNKS, n_tm - 1)),
                dma((CHUNKS, n_tm - 1)),
            ],
            compiler_params=pltpu.CompilerParams(
                collective_id=0, has_side_effects=True, vmem_limit_bytes=40 << 20
            ),
        )(returns, weights)

    in_specs = (P("tm", "paths", None), P("paths", None))
    out_specs = P("tm", "paths")
    return jax.shard_map(shards, mesh=mesh, in_specs=in_specs, out_specs=out_specs, check_vma=False)
```

time: 88.1 us -> 24.8 us (0.28)
  blocking collectives: 44.8 us -> 0 us
  other arithmetic: 22.5 us -> 0 us
  Pallas kernels: 0 us -> 19.9 us
  matrix products: 8.14 us -> 0 us
  local copies, waits for them, and re-layouts: 12.1 us -> 4.69 us
    all_gather x3 -> x0, blocking collectives: 36.9 us -> none  [the longest x2 21 us: prefix(): gathered = jax.tree.map(lambda a: lax.all_gather(a, axis), part)]
    another operation x1 -> x0, other arithmetic: 20.9 us -> none  [shards(): peaks = jnp.maximum(lax.cummax(values, axis=0), 0.0)]
    pallas_call x0 -> x1, Pallas kernels: none -> 19.9 us  [shards(): pl.pallas_call(functools.partial(kernel, n_tm, n_paths), out_shape=jax.Sh...]
    dot_general x2 -> x0, matrix products: 8.14 us -> none  [the longest x1 6.03 us: shards(): jnp.einsum('tpa,aq->tqp', returns, all_weights, preferred_element_type=jn...]
    all_to_all x1 -> x0, blocking collectives: 7.85 us -> none  [shards(): lax.all_to_all(blocks, 'tm', split_axis=0, concat_axis=0, tiled=True)]
    unnamed x11 -> x5, local copies, waits for them, and re-layouts: 11.7 us -> 4.69 us
    reduce_max x2 -> x0, other arithmetic: 1.55 us -> none  [the longest x1 0.93 us: shards(): falls = jnp.max(running - (prior_offset[None] + values), axis=0)]
where the time goes in v1:
time: 24.8 us; the launch traced here: 24.6 us
  Pallas kernels  19.9 us (80%)
  local copies, waits for them, and re-layouts  4.69 us (19%)
    pallas_call x1, Pallas kernels, shards(): pl.pallas_call(functools.partial(kernel, n_tm, n_paths), out_shape=jax.Sh...  19.9 us
    unnamed x5, local copies, waits for them, and re-layouts  4.69 us

profile of v1, /device:TPU:0, one launch (start us, length us, event | category | flops | bytes accessed | tf_op | source)
XLA Modules:
  0.0 24.6 jit_solution(9314024490284385958)
XLA Ops:
  0.0 0.0 copy-start
  0.0 3.4 %copy-done = bf16[32,512,256]{2,1,0:T(8,128)(2,1)S(1)} copy-done((bf16[32,512,256]{2,1,0:T(8,128)(2,1)S(1)}, bf16[32,512,256]{2,1,0:T(8,128)(2,1)}, u32[]{:S(2)}) %copy-start) | copy-done | bytes 8388632
  3.4 0.0 copy-start.1
  3.4 0.7 %copy-done.1 = bf16[32,64]{1,0:T(8,128)(2,1)S(1)} copy-done((bf16[32,64]{1,0:T(8,128)(2,1)S(1)}, bf16[32,64]{1,0:T(8,128)(2,1)}, u32[]{:S(2)}) %copy-start.1) | copy-done | bytes 4120
  4.1 19.9 %shard_map.28 = f32[16,512]{1,0:T(8,128)S(1)} custom-call(bf16[32,512,256]{2,1,0:T(8,128)(2,1)S(1)} %copy-done, bf16[32,64]{1,0:T(8,128)(2,1)S(1)} %copy-done.1), custom_call_target="tpu_custom_call" | custom-call | tf_op jit(solution)/shard_map/pallas_call | solution.py:148
  24.0 0.6 %copy.4 = f32[16,512]{1,0:T(8,128)} copy(f32[16,512]{1,0:T(8,128)S(1)} %shard_map.28) | data formatting | bytes 65536
Async XLA Ops:
  0.0 3.4 %copy-start = (bf16[32,512,256]{2,1,0:T(8,128)(2,1)S(1)}, bf16[32,512,256]{2,1,0:T(8,128)(2,1)}, u32[]{:S(2)}) copy-start(bf16[32,512,256]{2,1,0:T(8,128)(2,1)} %ret_hbm.1) | copy-start | bytes 25165828
  3.4 0.7 %copy-start.1 = (bf16[32,64]{1,0:T(8,128)(2,1)S(1)}, bf16[32,64]{1,0:T(8,128)(2,1)}, u32[]{:S(2)}) copy-start(bf16[32,64]{1,0:T(8,128)(2,1)} %w_ref.1) | copy-start | bytes 12292

commit v2 on v1

--- a/solution.py
+++ b/solution.py
@@ -9,27 +9,28 @@
 
 MESH = pl.DeviceIdType.MESH
 CHUNKS = 2
-GROUP = 8
 ROWS = 32
 
 
 def kernel(
-    n_tm, n_paths, ret_hbm, w_ref, out_ref,
-    ret, wbuf, prof, send, recv, load_sem, wsend_sem, wrecv_sem, send_sem, recv_sem,
+    n_tm, n_paths, ret_hbm, w_hbm, out_ref,
+    ret, w_ref, wbuf, prof, send, recv, load_sem, own_sem, wsend_sem, wrecv_sem, send_sem, recv_sem,
 ):
     steps, paths, assets = ret.shape
     ports = w_ref.shape[1]
     block = ports // n_tm
     width = paths // CHUNKS
     half = width // 2
-    groups = steps // GROUP
+    groups = 1
     tm = lax.axis_index("tm")
     me = lax.axis_index("paths")
 
     def load(c, g):
-        part = (pl.ds(g * GROUP, GROUP), pl.ds(c * width, width))
+        part = (pl.ds(g * steps, steps), pl.ds(c * width, width))
         return pltpu.make_async_copy(ret_hbm.at[part], ret.at[part], load_sem.at[c, g])
 
+    own = pltpu.make_async_copy(w_hbm, w_ref, own_sem)
+    own.start()
     for c in range(CHUNKS):
         for g in range(groups):
             load(c, g).start()
@@ -43,6 +44,7 @@
         pl.semaphore_signal(
             barrier, inc=1, device_id=(lax.rem(tm + d, n_tm), me), device_id_type=MESH
         )
+    own.wait()
     pl.semaphore_wait(barrier, n_paths - 1 + n_tm - 1)
 
     def weight_copy(d):
@@ -92,12 +94,12 @@
         second = pl.ds(c * width + half, half)
         for g in range(groups):
             load(c, g).wait()
-            when = pl.ds(g * GROUP, GROUP)
-            left = ret[when, first, :].reshape(GROUP * half, assets)
-            right = ret[when, second, :].reshape(GROUP * half, assets)
+            when = pl.ds(g * steps, steps)
+            left = ret[when, first, :].reshape(steps * half, assets)
+            right = ret[when, second, :].reshape(steps * half, assets)
             prof[c, when] = jnp.dot(
                 jnp.concatenate([left, right], axis=1), both, preferred_element_type=jnp.float32
-            ).reshape(GROUP, half, 2 * ports)
+            ).reshape(steps, half, 2 * ports)
         pieces = []
         for r in range(0, half, ROWS):
             value = prof[c, 0, pl.ds(r, ROWS)]
@@ -149,24 +151,26 @@
             functools.partial(kernel, n_tm, n_paths),
             out_shape=jax.ShapeDtypeStruct((block, paths), jnp.float32),
             in_specs=[
-                pl.BlockSpec(memory_space=pl.ANY),
-                pl.BlockSpec(memory_space=pltpu.VMEM),
+                pl.BlockSpec(memory_space=pltpu.HBM),
+                pl.BlockSpec(memory_space=pltpu.HBM),
             ],
             out_specs=pl.BlockSpec(memory_space=pltpu.VMEM),
             scratch_shapes=[
                 pltpu.VMEM((steps, paths, assets), returns.dtype),
+                pltpu.VMEM((share, ports), weights.dtype),
                 pltpu.VMEM((n_paths, share, ports), weights.dtype),
                 pltpu.VMEM((CHUNKS, steps, width // 2, 2 * ports), jnp.float32),
                 pltpu.VMEM((CHUNKS, n_tm, 4, block, width), jnp.float32),
                 pltpu.VMEM((CHUNKS, n_tm, 4, block, width), jnp.float32),
-                dma((CHUNKS, steps // GROUP)),
+                dma((CHUNKS, 1)),
+                dma,
                 dma((n_paths - 1,)),
                 dma((n_paths - 1,)),
                 dma((CHUNKS, n_tm - 1)),
                 dma((CHUNKS, n_tm - 1)),
             ],
             compiler_params=pltpu.CompilerParams(
-                collective_id=0, has_side_effects=True, vmem_limit_bytes=40 << 20
+                collective_id=0, has_side_effects=True, vmem_limit_bytes=63 << 20
             ),
         )(returns, weights)
 

time: 24.8 us -> 21.7 us (0.88)
  local copies, waits for them, and re-layouts: 4.69 us -> 1.38 us
  Pallas kernels: 19.9 us -> 20.2 us
    unnamed x5 -> x1, local copies, waits for them, and re-layouts: 4.69 us -> 1.38 us
    pallas_call x1, Pallas kernels: 19.9 us -> 20.2 us  [shards(): pl.pallas_call(functools.partial(kernel, n_tm, n_paths), out_shape=jax.Sh...]
where the time goes in v2:
time: 21.7 us; the launch traced here: 21.6 us
  Pallas kernels  20.2 us (93%)
  local copies, waits for them, and re-layouts  1.38 us (6%)
    pallas_call x1, Pallas kernels, shards(): pl.pallas_call(functools.partial(kernel, n_tm, n_paths), out_shape=jax.Sh...  20.2 us
    unnamed x1, local copies, waits for them, and re-layouts  1.38 us

profile of v2, /device:TPU:0, one launch (start us, length us, event | category | flops | bytes accessed | tf_op | source)
XLA Modules:
  0.0 21.6 jit_solution(2489891606481771376)
XLA Ops:
  0.0 20.2 %shard_map.28 = f32[16,512]{1,0:T(8,128)} custom-call(bf16[32,512,256]{2,1,0:T(8,128)(2,1)} %ret_hbm.1, bf16[32,64]{1,0:T(8,128)(2,1)} %w_hbm.1), custom_call_target="tpu_custom_call" | custom-call | tf_op jit(solution)/shard_map/pallas_call | solution.py:150
  20.2 1.4 %copy.4 = f32[16,512]{1,0:T(8,128)} copy(f32[16,512]{1,0:T(8,128)} %shard_map.28) | data formatting | bytes 65536
